TPU v7x, 32 devices: a whole 2x2x4 slice. The times are simulated.
32 devices in a mesh: dp: 4 (over y, core), head: 2 (over x), kv: 4 (over z).
Axes of the slice: x: 2, y: 2, z: 4, core: 2. Of those that a mesh axis runs over, the one named last changes fastest.
Arguments:
- teacher_query: bfloat16 [4, 1024, 3584], P('dp', 'kv', 'head'), may hold values from -96 to 96
- teacher_key: bfloat16 [4, 1024, 512], P('dp', 'kv', 'head'), may hold values from -8 to 8
- student_query: bfloat16 [4, 1024, 1792], P('dp', 'kv', 'head'), may hold values from -96 to 96
- student_key: bfloat16 [4, 1024, 256], P('dp', 'kv', 'head'), may hold values from -8 to 8
- pair_table: int32 [14, 2], replicated, may hold values from 0 to 27, as said below
Outputs:
- kl: float32 [4, 14, 1024], P('dp', 'head', 'kv')
- head_loss: float32 [14], P('head')
Inputs may be any that keep to these rules, and one draw needn't show every extreme that they name: `pair_table`: each of the 28 teacher heads appears exactly once in the table.
All inputs are finite; a program needn't handle non-finite values.
Results may differ from a plain program's by a relative error of at most 0.0003.
Values may be sent and summed in bfloat16 or wider, within the bound.
A program may use at most 64 MiB of HBM per device.

v0:
```python
import math
import jax
import jax.numpy as jnp
from jax import lax
from jax.sharding import PartitionSpec as P

HT = 28
KVT = 4
DH = 128
HS = 14
KVS = 2
masked_value = -1e30


def running_softmax(running_max, running_total, logits, causal_mask):
    filled = jnp.where(causal_mask, logits, masked_value)
    new_max = jnp.maximum(running_max, jnp.max(filled, axis=-1))
    rescale = jnp.exp(running_max - new_max)
    weights = jnp.where(causal_mask, jnp.exp(filled - new_max[..., None]), 0.0)
    return (new_max, running_total * rescale + jnp.sum(weights, axis=-1), rescale, weights)


def make_fold(teacher_heads, teacher_select, student_heads, student_select, repeat, query_pos):
    seq_dev, row_count, pair_count, head_dim = teacher_heads.shape
    student_count = student_heads.shape[2]
    scale = 1.0 / math.sqrt(head_dim)
    last_query = query_pos[row_count - 1]

    def fold_step(carry, pieces, start):
        teacher_keys, student_keys = pieces
        key_count = teacher_keys.shape[1]
        block_size = math.gcd(key_count, 512)
        block_total = key_count // block_size
        visible = jnp.clip(last_query // block_size + 1, 0, block_total)

        def one_block(block_index, state):
            t_max, t_total, t_cross, s_max, s_total = state
            offset = block_index * block_size
            t_block = lax.dynamic_slice_in_dim(teacher_keys, offset, block_size, 1).reshape(
                seq_dev, block_size, -1, head_dim
            )
            s_block = lax.dynamic_slice_in_dim(student_keys, offset, block_size, 1).reshape(
                seq_dev, block_size, -1, head_dim
            )
            t_keys = jnp.take(t_block, teacher_select, axis=2)
            s_keys = jnp.take(s_block, student_select, axis=2)
            t_logits = (
                jnp.einsum(
                    "bqpd,bkpd->bpqk", teacher_heads, t_keys, preferred_element_type=jnp.float32
                )
                * scale
            )
            s_logits = (
                jnp.einsum(
                    "bqsd,bksd->bsqk", student_heads, s_keys, preferred_element_type=jnp.float32
                )
                * scale
            )
            key_pos = offset + jnp.arange(block_size, dtype=jnp.int32)
            causal_mask = key_pos[None, :] <= query_pos[:, None]
            t_max, t_total, t_rescale, t_weights = running_softmax(
                t_max, t_total, t_logits, causal_mask
            )
            s_max, s_total, s_rescale, s_weights = running_softmax(
                s_max, s_total, s_logits, causal_mask
            )
            split_logits = t_logits.reshape(seq_dev, student_count, repeat, row_count, block_size)
            gap = (split_logits - s_logits[:, :, None]).reshape(
                seq_dev, pair_count, row_count, block_size
            )
            t_cross = t_cross * t_rescale + jnp.sum(t_weights * gap, axis=-1)
            return (t_max, t_total, t_cross, s_max, s_total)

        return lax.fori_loop(0, visible, one_block, carry)

    pair_shape = (seq_dev, pair_count, row_count)
    student_shape = (seq_dev, student_count, row_count)
    initial = (
        jnp.full(pair_shape, masked_value, jnp.float32),
        jnp.zeros(pair_shape, jnp.float32),
        jnp.zeros(pair_shape, jnp.float32),
        jnp.full(student_shape, masked_value, jnp.float32),
        jnp.zeros(student_shape, jnp.float32),
    )
    return (fold_step, initial)


def finish_pairs(state, repeat):
    t_max, t_total, t_cross, s_max, s_total = state
    seq_dev, pair_count, row_count = t_max.shape
    student_count = s_max.shape[1]
    t_lse = t_max + jnp.log(t_total)
    s_lse = s_max + jnp.log(s_total)
    s_paired = jnp.broadcast_to(
        s_lse[:, :, None], (seq_dev, student_count, repeat, row_count)
    ).reshape(seq_dev, pair_count, row_count)
    return t_cross / t_total - t_lse + s_paired


def per_device(teacher_query, teacher_key, student_query, student_key, pair_table):
    seq_dev, row_count, teacher_width = teacher_query.shape
    n_head = lax.axis_size("head")
    n_kv = lax.axis_size("kv")
    n_data = lax.axis_size("dp")
    head_index = lax.axis_index("head")
    kv_index = lax.axis_index("kv")
    group_teacher = HT // KVT
    group_student = HS // KVS
    local_student = HS // n_head
    local_student_kv = KVS // n_head
    query_pos = kv_index * row_count + jnp.arange(row_count, dtype=jnp.int32)
    all_tq, all_tk = (
        lax.all_gather(teacher_query, "head", axis=2, tiled=True),
        lax.all_gather(teacher_key, "head", axis=2, tiled=True),
    )
    my_pairs = lax.dynamic_slice_in_dim(
        pair_table, head_index * local_student, local_student, 0
    ).reshape(-1)
    teacher_heads = jnp.take(all_tq.reshape(seq_dev, row_count, HT, DH), my_pairs, axis=2)
    teacher_select = my_pairs // group_teacher
    student_heads = student_query.reshape(seq_dev, row_count, local_student, DH)
    student_ids = head_index * local_student + jnp.arange(local_student, dtype=jnp.int32)
    student_select = student_ids // group_student - head_index * local_student_kv
    fold_step, initial = make_fold(
        teacher_heads, teacher_select, student_heads, student_select, 2, query_pos
    )
    state = fold_step(
        initial,
        (
            lax.all_gather(all_tk, "kv", axis=1, tiled=True),
            lax.all_gather(student_key, "kv", axis=1, tiled=True),
        ),
        jnp.int32(0),
    )
    pair_kl = finish_pairs(state, 2)
    kl_local = jnp.sum(pair_kl.reshape(seq_dev, local_student, 2, row_count), axis=2)
    head_sums = jnp.sum(kl_local, axis=(0, 2))
    total = lax.psum(head_sums, ("dp", "kv"))
    head_loss = total / (seq_dev * n_data * row_count * n_kv)
    return (kl_local, head_loss)


def solution(mesh):
    in_specs = (
        P("dp", "kv", "head"),
        P("dp", "kv", "head"),
        P("dp", "kv", "head"),
        P("dp", "kv", "head"),
        P(),
    )
    out_specs = (P("dp", "head", "kv"), P("head"))
    return jax.shard_map(
        per_device, mesh=mesh, in_specs=in_specs, out_specs=out_specs, check_vma=False
    )
```

profile of v0, /device:TPU:0, one launch (start us, length us, event | category | flops | bytes accessed | tf_op | source)
XLA Modules:
  0.0 131.6 jit_solution(168695083922571773)
XLA Ops:
  7.2 0.0 copy-start
  7.2 0.0 copy-start.1
  7.2 0.0 copy-start.2
  7.2 0.0 all-gather.5.cloned.1.call-start
  7.2 2.3 %copy.18 = bf16[1,256,1792]{1,2,0:T(8,128)(2,1)} copy(bf16[1,256,1792]{2,1,0:T(8,128)(2,1)} %param.7) | data formatting | bytes 1835008 | tf_op args[0]
  9.5 0.0 all-gather.5.cloned.1.call-update
  9.5 0.0 all-gather.3.cloned.1.call-start
  9.6 1.0 copy.17
  10.6 7.2 %all_gather.12 = bf16[1,256,512]{1,2,0:T(8,128)(2,1)} all-gather(bf16[1,256,256]{1,2,0:T(8,128)(2,1)S(1)} %copy.17), channel_id=1, replica_groups=mesh['dp'=4,'head'=2,'kv'=4] {'head'}, dimensions={2}, use_global_device_ids=true | all-gather | bytes 393216 | tf_op jit(solution)/shard_map/all_gather | solution.py:114
  17.8 0.0 all-gather.3.cloned.1.call-update
  17.9 0.6 slice.3
  20.1 0.0 copy-done
  20.1 0.1 constant_dynamic-slice_fusion.1
  20.2 0.1 copy.16
  20.2 0.1 reshape.172
  20.3 0.1 reshape.174
  21.0 0.0 copy-done.1
  21.0 0.2 copy.21
  21.2 0.3 copy.22
  21.5 0.0 copy-done.2
  21.5 14.4 %all_gather.15 = bf16[1,1024,128]{2,1,0:T(8,128)(2,1)S(1)} all-gather(bf16[1,256,128]{2,1,0:T(8,128)(2,1)S(1)} %copy-done.2), channel_id=1, replica_groups=mesh['dp'=4,'head'=2,'kv'=4] {'kv'}, dimensions={1}, use_global_device_ids=true | all-gather | bytes 327680 | tf_op jit(solution)/shard_map/all_gather | solution.py:131
  35.9 6.6 %all-gather.5.cloned.1.call-done = bf16[1,256,3584]{1,2,0:T(8,128)(2,1)} async-done(((bf16[1,256,1792]{1,2,0:T(8,128)(2,1)}), bf16[1,256,3584]{1,2,0:T(8,128)(2,1)}) %all-gather.5.cloned.1.call-update) | async-done | bytes 1835024 | tf_op jit(solution)/shard_map/all_gather | solution.py:113
  42.5 2.9 %copy.20 = bf16[256,28,128]{2,0,1:T(8,128)(2,1)S(1)} copy(bf16[256,28,128]{0,2,1:T(8,128)(2,1)} %bitcast.99) | data formatting | bytes 3670016 | tf_op jit(solution)/shard_map/reshape | solution.py:119
  45.4 0.7 gather_fusion.1
  46.2 1.1 bitcast_select_fusion.1
  47.3 26.8 %all-gather.3.cloned.1.call-done = bf16[1,1024,512]{1,2,0:T(8,128)(2,1)} async-done(((bf16[1,256,512]{1,2,0:T(8,128)(2,1)}), bf16[1,1024,512]{1,2,0:T(8,128)(2,1)}) %all-gather.3.cloned.1.call-update) | async-done | bytes 1048592 | tf_op jit(solution)/shard_map/all_gather | solution.py:130
  74.1 9.4 %while.19 = (s32[]{:T(128)}, f32[1,14,256]{2,1,0:T(8,128)S(1)}, f32[1,14,256]{2,1,0:T(8,128)S(1)}, f32[1,14,256]{2,1,0:T(8,128)S(1)}, f32[1,7,256]{2,1,0:T(8,128...) while((s32[]{:T(128)}, f32[1,14,256]{2,1,0:T(8,128)S(1)}, ...), condition=%wide.region_6.7_spmd.clone, body=%wide.region_0.6_spmd.clone.sunk | while | flops 732774400 | bytes 36064820 | solution.py:74
  74.1 1.1 constant_dynamic-slice_fusion.3
  75.2 0.3 copy.24
  75.5 0.9 gather_fusion
  76.4 0.1 broadcast_compare_fusion.2
  76.6 2.6 %fusion.28 = (f32[14,256]{1,0:T(8,128)S(1)}, f32[14,512,256]{2,1,0:T(8,128)S(1)}) fusion(pred[256,512]{0,1:T(8,128)(4,1)S(1)} %broadcast_compare_fusion.2, bf16[1,256,14,128]{3,1,2,0:T(8,128)(2,1)} %get-tuple-element.346, bf16[14,512,128]{2,1,0:T(8,128)(2,1)S(1)} %gather_fusion, pred[14]{0:T(512)(128)(4,1)S(1)} %compare_and_fusion.5), kind=kOutput, calls=%fused_computation.9.clone.1 | convolution fusion | flops 476180992 | bytes 10237966 | tf_op jit(solution)/shard_map/while/body/bqpd,bkpd->bpqk/dot_general | solution.py:48
  79.3 0.8 select_reduce_fusion.4
  80.1 2.6 %fusion.29 = (f32[14,256]{1,0:T(8,128)S(1)}, f32[14,256]{1,0:T(8,128)S(1)}) fusion(f32[14,512,256]{2,1,0:T(8,128)S(1)} %get-tuple-element.292, f32[7,256,512]{1,2,0:T(8,128)S(1)} %get-tuple-element.293, f32[14,256]{1,0:T(8,128)S(1)} %bitcast.97, pred[256,512]{0,1:T(8,128)(4,1)S(1)} %broadcast_compare_fusion.2), kind=kLoop, calls=%fused_computation.6.clone.1 | loop fusion | flops 14672896 | bytes 11184128 | tf_op jit(solution)/shard_map/while/body/reduce_sum | solution.py:71
  82.7 0.8 select_reduce_fusion.5
  83.6 0.1 fusion.23
  83.7 0.1 reduce_sum.63
  83.8 0.1 reduce_sum.64
  83.9 0.6 reduce_sum.61
  84.5 39.7 %psum.7 = f32[7]{0:T(128)S(1)} all-reduce(f32[7]{0:T(128)S(1)} %reduce_sum.64), channel_id=1, replica_groups=mesh['dp'=4,'head'=2,'kv'=4] {'dp','kv'}, use_global_device_ids=true, to_apply=%region_10.11 | all-reduce | flops 7 | bytes 56 | tf_op jit(solution)/shard_map/psum | solution.py:138
  124.3 0.5 broadcast_multiply_fusion
  (28 shorter events, 0.2 us)
Async XLA Ops:
  7.2 12.9 %copy-start = (s32[14,2]{0,1:T(2,128)S(1)}, s32[14,2]{0,1:T(2,128)}, u32[]{:S(2)}) copy-start(s32[14,2]{0,1:T(2,128)} %param.11) | copy-start | bytes 340
  7.2 13.8 %copy-start.1 = (bf16[1,256,896]{2,1,0:T(8,128)(2,1)S(1)}, bf16[1,256,896]{2,1,0:T(8,128)(2,1)}, u32[]{:S(2)}) copy-start(bf16[1,256,896]{2,1,0:T(8,128)(2,1)} %param.9) | copy-start | bytes 1376260
  7.2 14.3 %copy-start.2 = (bf16[1,256,128]{2,1,0:T(8,128)(2,1)S(1)}, bf16[1,256,128]{2,1,0:T(8,128)(2,1)}, u32[]{:S(2)}) copy-start(bf16[1,256,128]{2,1,0:T(8,128)(2,1)} %param.10) | copy-start | bytes 196612
  7.2 35.3 %all-gather.5.cloned.1.call-start = ((), (), s32[]{:S(2)}) async-start(), calls=%async_computation.1 | async-start | bytes 2752512 | tf_op jit(solution)/shard_map/all_gather | solution.py:113
  9.5 64.5 %all-gather.3.cloned.1.call-start = ((), (), s32[]{:S(2)}) async-start(), calls=%async_computation | async-start | bytes 1310720 | tf_op jit(solution)/shard_map/all_gather | solution.py:130
Sparse Core Ops, SparseCore 0:
  9.7 32.8 all-gather.4
  44.1 29.9 all-gather.2
where the time goes:
time: 132 us
  blocking collectives  61.4 us (47%)
  waiting for transfers between devices  33.5 us (25%)
  between operations  16.4 us (12%)
  local copies, waits for them, and re-layouts  11.3 us (9%)
  other arithmetic  5.49 us (4%)
  matrix products  3.37 us (3%)
    psum x1, blocking collectives, per_device(): total = lax.psum(head_sums, ('dp', 'kv'))  39.7 us
    all_gather x1, waiting for transfers between devices, per_device(): lax.all_gather(all_tk, 'kv', axis=1, tiled=True)  26.8 us
    all_gather x1, blocking collectives, per_device(): lax.all_gather(student_key, 'kv', axis=1, tiled=True)  14.4 us
    all_gather x1, blocking collectives, per_device(): lax.all_gather(teacher_key, 'head', axis=2, tiled=True)  7.22 us
    all_gather x1, waiting for transfers between devices, per_device(): lax.all_gather(teacher_query, 'head', axis=2, tiled=True)  6.6 us
    unnamed x10, local copies, waits for them, and re-layouts  3.76 us
    reshape x1, local copies, waits for them, and re-layouts, per_device(): all_tq.reshape(seq_dev, row_count, HT, DH)  2.89 us
  transfers between devices with their start and end apart: 2, of which 2 were waited for; matrix products, arithmetic and copies ran while one was open for 5% of the time, Pallas kernels for 0%

commit v1 on v0

--- a/solution.py
+++ b/solution.py
@@ -10,6 +10,12 @@
 HS = 14
 KVS = 2
 masked_value = -1e30
+
+
+def stack_and_merge(x, axis, dim):
+    terms = lax.all_gather(x, axis, axis=0, tiled=False)
+    result = jnp.concatenate(terms, axis=dim)
+    return result
 
 
 def running_softmax(running_max, running_total, logits, causal_mask):
@@ -111,7 +117,7 @@
     query_pos = kv_index * row_count + jnp.arange(row_count, dtype=jnp.int32)
     all_tq, all_tk = (
         lax.all_gather(teacher_query, "head", axis=2, tiled=True),
-        lax.all_gather(teacher_key, "head", axis=2, tiled=True),
+        stack_and_merge(teacher_key, "head", 2),
     )
     my_pairs = lax.dynamic_slice_in_dim(
         pair_table, head_index * local_student, local_student, 0

time: 132 us -> 132 us (level)
    unnamed x10 -> x9, local copies, waits for them, and re-layouts: 3.76 us -> 2.76 us
where the time goes in v1:
time: 132 us
  blocking collectives  61.5 us (47%)
  waiting for transfers between devices  33.5 us (25%)
  between operations  16.4 us (12%)
  local copies, waits for them, and re-layouts  11.1 us (8%)
  other arithmetic  5.49 us (4%)
  matrix products  3.37 us (3%)
    psum x1, blocking collectives, per_device(): total = lax.psum(head_sums, ('dp', 'kv'))  39.7 us
    all_gather x1, waiting for transfers between devices, per_device(): lax.all_gather(all_tk, 'kv', axis=1, tiled=True)  26.8 us
    all_gather x1, blocking collectives, per_device(): lax.all_gather(student_key, 'kv', axis=1, tiled=True)  14.3 us
    all_gather x1, blocking collectives, stack_and_merge(): terms = lax.all_gather(x, axis, axis=0, tiled=False)  7.39 us
    all_gather x1, waiting for transfers between devices, per_device(): lax.all_gather(teacher_query, 'head', axis=2, tiled=True)  6.68 us
    reshape x1, local copies, waits for them, and re-layouts, per_device(): all_tq.reshape(seq_dev, row_count, HT, DH)  2.89 us
    unnamed x9, local copies, waits for them, and re-layouts  2.76 us
  transfers between devices with their start and end apart: 2, of which 2 were waited for; matrix products, arithmetic and copies ran while one was open for 5% of the time, Pallas kernels for 0%

profile of v1, /device:TPU:0, one launch (start us, length us, event | category | flops | bytes accessed | tf_op | source)
XLA Modules:
  0.0 131.6 jit_solution(8342393406558869494)
XLA Ops:
  7.2 0.0 copy-start
  7.2 0.0 copy-start.1
  7.2 0.0 copy-start.2
  7.2 0.0 all-gather.6.cloned.1.call-start
  7.2 2.3 %copy.35 = bf16[1,256,1792]{1,2,0:T(8,128)(2,1)} copy(bf16[1,256,1792]{2,1,0:T(8,128)(2,1)} %param.7) | data formatting | bytes 1835008 | tf_op args[0]
  9.5 0.0 all-gather.6.cloned.1.call-update
  9.5 0.0 all-gather.4.cloned.1.call-start
  9.6 7.4 %all-gather = bf16[2,256,256]{2,1,0:T(8,128)(2,1)S(1)} all-gather(bf16[1,256,256]{2,1,0:T(8,128)(2,1)} %param.8), channel_id=2, replica_groups=mesh['dp'=4,'head'=2,'kv'=4] {'head'}, dimensions={0}, use_global_device_ids=true | all-gather | bytes 393216 | tf_op jit(solution)/shard_map/all_gather | solution.py:16
  17.0 0.8 copy.34
  17.8 0.0 all-gather.4.cloned.1.call-update
  17.8 0.6 slice.3
  20.1 0.0 copy-done
  20.1 0.1 constant_dynamic-slice_fusion.1
  20.1 0.1 copy.33
  20.2 0.1 reshape.178
  20.3 0.1 reshape.182
  21.0 0.0 copy-done.1
  21.0 0.2 copy.38
  21.2 0.3 copy.39
  21.5 0.0 copy-done.2
  21.5 14.3 %all_gather.19 = bf16[1,1024,128]{2,1,0:T(8,128)(2,1)S(1)} all-gather(bf16[1,256,128]{2,1,0:T(8,128)(2,1)S(1)} %copy-done.2), channel_id=1, replica_groups=mesh['dp'=4,'head'=2,'kv'=4] {'kv'}, dimensions={1}, use_global_device_ids=true | all-gather | bytes 327680 | tf_op jit(solution)/shard_map/all_gather | solution.py:137
  35.9 6.7 %all-gather.6.cloned.1.call-done = bf16[1,256,3584]{1,2,0:T(8,128)(2,1)} async-done(((bf16[1,256,1792]{1,2,0:T(8,128)(2,1)}), bf16[1,256,3584]{1,2,0:T(8,128)(2,1)}) %all-gather.6.cloned.1.call-update) | async-done | bytes 1835024 | tf_op jit(solution)/shard_map/all_gather | solution.py:119
  42.5 2.9 %copy.37 = bf16[256,28,128]{2,0,1:T(8,128)(2,1)S(1)} copy(bf16[256,28,128]{0,2,1:T(8,128)(2,1)} %bitcast.104) | data formatting | bytes 3670016 | tf_op jit(solution)/shard_map/reshape | solution.py:125
  45.4 0.7 gather_fusion.1
  46.2 1.1 bitcast_select_fusion.1
  47.3 26.8 %all-gather.4.cloned.1.call-done = bf16[1,1024,512]{1,2,0:T(8,128)(2,1)} async-done(((bf16[1,256,512]{1,2,0:T(8,128)(2,1)}), bf16[1,1024,512]{1,2,0:T(8,128)(2,1)}) %all-gather.4.cloned.1.call-update) | async-done | bytes 1048592 | tf_op jit(solution)/shard_map/all_gather | solution.py:136
  74.1 9.4 %while.19 = (s32[]{:T(128)}, f32[1,14,256]{2,1,0:T(8,128)S(1)}, f32[1,14,256]{2,1,0:T(8,128)S(1)}, f32[1,14,256]{2,1,0:T(8,128)S(1)}, f32[1,7,256]{2,1,0:T(8,128...) while((s32[]{:T(128)}, f32[1,14,256]{2,1,0:T(8,128)S(1)}, ...), condition=%wide.region_6.7_spmd.clone, body=%wide.region_0.6_spmd.clone.sunk | while | flops 732774400 | bytes 36064820 | solution.py:80
  74.1 1.1 constant_dynamic-slice_fusion.3
  75.2 0.3 copy.41
  75.5 0.9 gather_fusion
  76.4 0.1 broadcast_compare_fusion.2
  76.6 2.6 %fusion.28 = (f32[14,256]{1,0:T(8,128)S(1)}, f32[14,512,256]{2,1,0:T(8,128)S(1)}) fusion(pred[256,512]{0,1:T(8,128)(4,1)S(1)} %broadcast_compare_fusion.2, bf16[1,256,14,128]{3,1,2,0:T(8,128)(2,1)} %get-tuple-element.376, bf16[14,512,128]{2,1,0:T(8,128)(2,1)S(1)} %gather_fusion, pred[14]{0:T(512)(128)(4,1)S(1)} %compare_and_fusion.5), kind=kOutput, calls=%fused_computation.9.clone.1 | convolution fusion | flops 476180992 | bytes 10237966 | tf_op jit(solution)/shard_map/while/body/bqpd,bkpd->bpqk/dot_general | solution.py:54
  79.3 0.8 select_reduce_fusion.4
  80.1 2.6 %fusion.29 = (f32[14,256]{1,0:T(8,128)S(1)}, f32[14,256]{1,0:T(8,128)S(1)}) fusion(f32[14,512,256]{2,1,0:T(8,128)S(1)} %get-tuple-element.322, f32[7,256,512]{1,2,0:T(8,128)S(1)} %get-tuple-element.323, f32[14,256]{1,0:T(8,128)S(1)} %bitcast.102, pred[256,512]{0,1:T(8,128)(4,1)S(1)} %broadcast_compare_fusion.2), kind=kLoop, calls=%fused_computation.6.clone.1 | loop fusion | flops 14672896 | bytes 11184128 | tf_op jit(solution)/shard_map/while/body/reduce_sum | solution.py:77
  82.7 0.8 select_reduce_fusion.5
  83.6 0.1 fusion.23
  83.7 0.1 reduce_sum.63
  83.8 0.1 reduce_sum.64
  83.9 0.6 reduce_sum.61
  84.5 39.7 %psum.7 = f32[7]{0:T(128)S(1)} all-reduce(f32[7]{0:T(128)S(1)} %reduce_sum.64), channel_id=1, replica_groups=mesh['dp'=4,'head'=2,'kv'=4] {'dp','kv'}, use_global_device_ids=true, to_apply=%region_10.11 | all-reduce | flops 7 | bytes 56 | tf_op jit(solution)/shard_map/psum | solution.py:144
  124.3 0.5 broadcast_multiply_fusion
  (28 shorter events, 0.2 us)
Async XLA Ops:
  7.2 12.9 %copy-start = (s32[14,2]{0,1:T(2,128)S(1)}, s32[14,2]{0,1:T(2,128)}, u32[]{:S(2)}) copy-start(s32[14,2]{0,1:T(2,128)} %param.11) | copy-start | bytes 340
  7.2 13.8 %copy-start.1 = (bf16[1,256,896]{2,1,0:T(8,128)(2,1)S(1)}, bf16[1,256,896]{2,1,0:T(8,128)(2,1)}, u32[]{:S(2)}) copy-start(bf16[1,256,896]{2,1,0:T(8,128)(2,1)} %param.9) | copy-start | bytes 1376260
  7.2 14.3 %copy-start.2 = (bf16[1,256,128]{2,1,0:T(8,128)(2,1)S(1)}, bf16[1,256,128]{2,1,0:T(8,128)(2,1)}, u32[]{:S(2)}) copy-start(bf16[1,256,128]{2,1,0:T(8,128)(2,1)} %param.10) | copy-start | bytes 196612
  7.2 35.3 %all-gather.6.cloned.1.call-start = ((), (), s32[]{:S(2)}) async-start(), calls=%async_computation.1 | async-start | bytes 2752512 | tf_op jit(solution)/shard_map/all_gather | solution.py:119
  9.5 64.5 %all-gather.4.cloned.1.call-start = ((), (), s32[]{:S(2)}) async-start(), calls=%async_computation | async-start | bytes 1310720 | tf_op jit(solution)/shard_map/all_gather | solution.py:136
Sparse Core Ops, SparseCore 0:
  9.7 32.8 all-gather.5
  44.1 29.9 all-gather.3
